TPU v7x, 32 devices: a whole 2x2x4 slice. The times are simulated.
32 devices in a mesh: layer: 4 (over z), facet: 8 (over y, x, core).
Axes of the slice: x: 2, y: 2, z: 4, core: 2. Of those that a mesh axis runs over, the one named last changes fastest.
Arguments:
- model_strip: bfloat16 [8, 2, 64, 8192], P('facet', None, None, 'layer'), may hold values from -6 to 6
- screen_angle: bfloat16 [4, 8, 64, 8192], P('layer', 'facet'), may hold values from -3.140625 to 3.140625
- facet_window: float32 [8, 8192], P('facet'), may hold values from 0.04 to 0.16
- facet_shift: int32 [8], P('facet'), may hold values from 0 to 8191
- kernel_taps: float32 [7], replicated, may hold values from 0.2 to 0.6
- plane_angle: float32 [4, 8], P('layer'), may hold values from -3.140625 to 3.140625
- u_cell: int32 [4, 128, 512], P('layer', 'facet'), may hold values from 0 to 63
- v_cell: int32 [4, 128, 512], P('layer', 'facet'), may hold values from 0 to 63
- w_plane: int32 [4, 128, 512], P('layer', 'facet'), may hold values from 0 to 7
- observed: float32 [4, 128, 2, 512], P('layer', 'facet'), may hold values from -6 to 6
Outputs:
- residual: float32 [4, 128, 2, 512], P('layer', 'facet')
- gradient: float32 [8, 2, 64, 8192], P('facet', None, None, 'layer')
All inputs are finite; a program needn't handle non-finite values.
Results may differ from a plain program's by a relative error of at most 0.009.
Values may be sent and summed in bfloat16 or wider, within the bound.
A program may use at most 64 MiB of HBM per device.

v0:
```python
import math
import jax
import jax.numpy as jnp
from jax import lax
from jax.sharding import PartitionSpec as P

STRIP_LEN = 8192
SUB_ROWS = 64
STRIP_COLS = 64
PLANES = 8
SUBGRIDS = 128
back_gain = 8.0


def fourier_table(length):
    positions = jnp.arange(length, dtype=jnp.int32)
    turn_count = positions[:, None] * positions[None, :] % length
    angles = 2.0 * math.pi / length * turn_count.astype(jnp.float32)
    norm_scale = 1.0 / math.sqrt(length)
    return (jnp.stack([jnp.cos(angles), -jnp.sin(angles)]) * norm_scale).astype(jnp.bfloat16)


def twiddle():
    low_index = jnp.arange(SUB_ROWS, dtype=jnp.int32)
    high_index = jnp.arange(SUBGRIDS, dtype=jnp.int32)
    turn_count = low_index[:, None] * high_index[None, :] % STRIP_LEN
    angles = 2.0 * math.pi / STRIP_LEN * turn_count.astype(jnp.float32)
    return (jnp.cos(angles), -jnp.sin(angles))


def facet_factor(window, shift_cells):
    positions = jnp.arange(STRIP_LEN, dtype=jnp.int32)
    turn_count = positions * shift_cells % STRIP_LEN
    angles = 2.0 * math.pi / STRIP_LEN * turn_count.astype(jnp.float32)
    factor_real = (window * jnp.cos(angles)).reshape(SUBGRIDS, SUB_ROWS, 1)
    factor_imag = (-window * jnp.sin(angles)).reshape(SUBGRIDS, SUB_ROWS, 1)
    return (factor_real, factor_imag)


def forward(screened, window, shift_cells):
    grid_view = screened.reshape(2, STRIP_COLS, SUB_ROWS, SUBGRIDS)
    section_one = jnp.einsum(
        "tka,pcab->tpckb", fourier_table(SUB_ROWS), grid_view, preferred_element_type=jnp.float32
    )
    real_part = section_one[0, 0] - section_one[1, 1]
    imag_part = section_one[0, 1] + section_one[1, 0]
    twist_real, twist_imag = twiddle()
    mixed = jnp.stack(
        [
            real_part * twist_real - imag_part * twist_imag,
            real_part * twist_imag + imag_part * twist_real,
        ]
    ).astype(jnp.bfloat16)
    section_two = jnp.einsum(
        "tjb,pckb->tpjkc", fourier_table(SUBGRIDS), mixed, preferred_element_type=jnp.float32
    )
    spec_real = section_two[0, 0] - section_two[1, 1]
    spec_imag = section_two[0, 1] + section_two[1, 0]
    factor_real, factor_imag = facet_factor(window, shift_cells)
    return jnp.concatenate(
        [
            spec_real * factor_real - spec_imag * factor_imag,
            spec_real * factor_imag + spec_imag * factor_real,
        ],
        axis=2,
    ).astype(jnp.bfloat16)


def backward(all_grids, window, shift_cells, screen_phase):
    values = all_grids.astype(jnp.float32)
    grid_real = values[:, :, :STRIP_COLS]
    grid_imag = values[:, :, STRIP_COLS:]
    factor_real, factor_imag = facet_factor(window, shift_cells)
    spectral = jnp.stack(
        [
            grid_real * factor_real + grid_imag * factor_imag,
            grid_imag * factor_real - grid_real * factor_imag,
        ]
    ).astype(jnp.bfloat16)
    section_two = jnp.einsum(
        "tjb,pjkc->tpckb", fourier_table(SUBGRIDS), spectral, preferred_element_type=jnp.float32
    )
    half_real = section_two[0, 0] + section_two[1, 1]
    half_imag = section_two[0, 1] - section_two[1, 0]
    twist_real, twist_imag = twiddle()
    mixed = jnp.stack(
        [
            half_real * twist_real + half_imag * twist_imag,
            half_imag * twist_real - half_real * twist_imag,
        ]
    ).astype(jnp.bfloat16)
    section_one = jnp.einsum(
        "tka,pckb->tpcab", fourier_table(SUB_ROWS), mixed, preferred_element_type=jnp.float32
    )
    image_real = (section_one[0, 0] + section_one[1, 1]).reshape(STRIP_COLS, STRIP_LEN)
    image_imag = (section_one[0, 1] - section_one[1, 0]).reshape(STRIP_COLS, STRIP_LEN)
    phases = screen_phase.astype(jnp.float32)
    cosine = jnp.cos(phases)
    sine_part = jnp.sin(phases)
    return back_gain * jnp.stack(
        [image_real * cosine + image_imag * sine_part, image_imag * cosine - image_real * sine_part]
    )


def spread(cell_index, length, kernel_taps):
    tap_count = kernel_taps.shape[0]
    offset = (jnp.arange(length, dtype=jnp.int32)[None, :] - cell_index[:, None]) % length
    wanted = (jnp.arange(tap_count, dtype=jnp.int32) - tap_count // 2) % length
    matches = (offset[:, :, None] == wanted[None, None, :]).astype(jnp.float32)
    return jnp.sum(matches * kernel_taps, axis=2)


def adjoint_from(row_weights, column_weights, weighted):
    spread_cols = jnp.concatenate(
        [weighted[0][:, None] * column_weights, weighted[1][:, None] * column_weights], axis=1
    )
    return jnp.dot(row_weights.T, spread_cols, precision=lax.Precision.HIGHEST)


def degrid(subgrid, row_cells, column_cells, plane, observed_vis, angle_table, kernel_taps):
    row_weights = spread(row_cells, SUB_ROWS, kernel_taps)
    column_weights = spread(column_cells, STRIP_COLS, kernel_taps)
    kernel_rows = jnp.dot(row_weights, subgrid, precision=lax.Precision.HIGHEST)
    model_real = jnp.sum(kernel_rows[:, :STRIP_COLS] * column_weights, axis=1)
    model_imag = jnp.sum(kernel_rows[:, STRIP_COLS:] * column_weights, axis=1)
    plane_pick = (plane[:, None] == jnp.arange(PLANES, dtype=jnp.int32)[None, :]).astype(
        jnp.float32
    )
    phase_angle = jnp.sum(plane_pick * angle_table[None, :], axis=1)
    cosine = jnp.cos(phase_angle)
    sine_part = jnp.sin(phase_angle)
    residual_real = observed_vis[0] - (model_real * cosine - model_imag * sine_part)
    residual_imag = observed_vis[1] - (model_real * sine_part + model_imag * cosine)
    weighted = jnp.stack(
        [
            residual_real * cosine + residual_imag * sine_part,
            residual_imag * cosine - residual_real * sine_part,
        ]
    )
    return (jnp.stack([residual_real, residual_imag]), weighted, row_weights, column_weights)


def local(
    model_strip,
    screen_angle,
    facet_window,
    facet_shift,
    kernel_taps,
    plane_angle,
    u_cell,
    v_cell,
    w_plane,
    observed,
):
    strip_data = lax.all_gather(model_strip, "layer", axis=3, tiled=True)[0]
    phases = screen_angle[0, 0].astype(jnp.float32)
    cosine = jnp.cos(phases)
    sine_part = jnp.sin(phases)
    strip_values = strip_data.astype(jnp.float32)
    screened = jnp.stack(
        [
            strip_values[0] * cosine - strip_values[1] * sine_part,
            strip_values[0] * sine_part + strip_values[1] * cosine,
        ]
    ).astype(jnp.bfloat16)
    contrib = forward(screened, facet_window[0], facet_shift[0])
    received = lax.all_to_all(contrib, "facet", split_axis=0, concat_axis=0, tiled=True)
    owner_count = lax.axis_size("facet")
    per_owner = received.shape[0] // owner_count
    grids = jnp.sum(
        received.reshape(owner_count, per_owner, SUB_ROWS, 2 * STRIP_COLS).astype(jnp.float32),
        axis=0,
    )
    residual_vis, weighted, row_weights, column_weights = jax.vmap(
        degrid, in_axes=(0, 0, 0, 0, 0, None, None)
    )(grids, u_cell[0], v_cell[0], w_plane[0], observed[0], plane_angle[0], kernel_taps)
    adjoint = jax.vmap(adjoint_from)(row_weights, column_weights, weighted).astype(jnp.bfloat16)
    all_grids = lax.all_gather(adjoint, "facet", axis=0, tiled=True)
    term = backward(all_grids, facet_window[0], facet_shift[0], screen_angle[0, 0]).astype(
        jnp.bfloat16
    )
    pieces = lax.all_to_all(term[None], "layer", split_axis=3, concat_axis=0, tiled=True)
    gradient = jnp.sum(pieces.astype(jnp.float32), axis=0)[None]
    return (residual_vis[None], gradient)


def solution(mesh):
    return jax.shard_map(
        local,
        mesh=mesh,
        in_specs=(
            P("facet", None, None, "layer"),
            P("layer", "facet", None, None),
            P("facet", None),
            P("facet"),
            P(),
            P("layer", None),
            P("layer", "facet", None),
            P("layer", "facet", None),
            P("layer", "facet", None),
            P("layer", "facet", None, None),
        ),
        out_specs=(P("layer", "facet", None, None), P("facet", None, None, "layer")),
        check_vma=False,
    )
```

profile of v0, /device:TPU:0, one launch (start us, length us, event | category | flops | bytes accessed | tf_op | source)
XLA Modules:
  0.0 259.3 jit_solution(13630020163129976060)
XLA Ops:
  13.0 45.0 %all-gather.3.cloned.1.call-done = bf16[1,2,64,8192]{3,2,1,0:T(8,128)(2,1)} async-done(((bf16[1,2,64,2048]{3,2,1,0:T(8,128)(2,1)}), bf16[1,2,64,8192]{3,2,1,0:T(8,128)(2,1)}) %all-gather.3.cloned.1.call-update) | async-done | bytes 2097168 | tf_op jit(solution)/shard_map/all_gather | solution.py:155
  58.0 2.0 convert_element_type.143
  60.0 8.0 %fusion.51 = (bf16[8,8,64,128]{3,1,2,0:T(8,128)(2,1)S(1)}, bf16[8,8,64,128]{3,1,2,0:T(8,128)(2,1)S(1)}) fusion(f32[1,2,64,8192]{3,2,1,0:T(8,128)S(1)} %convert_element_type.143, bf16[1,1,64,8192]{3,2,1,0:T(8,128)(2,1)S(1)} %copy-done.2), kind=kLoop, calls=%fused_computation.93 | loop fusion | flops 4718592 | bytes 7340032
  73.4 3.4 %copy.96 = bf16[128,64,128]{2,1,0:T(8,128)(2,1)} copy(bf16[128,64,128]{0,1,2:T(8,128)(2,1)S(1)} %pad_maximum_fusion) | data formatting | bytes 4194304 | tf_op jit(solution)/shard_map/concatenate | solution.py:60
  76.8 4.5 %all-to-all-start = ((bf16[128,64,128]{2,1,0:T(8,128)(2,1)}), bf16[128,64,128]{2,1,0:T(8,128)(2,1)}, u32[]{:S(2)}, u32[]{:S(2)}) async-start(bf16[128,64,128]{2,1,0:T(8,128)(2,1)} %copy.96), calls=%async_computation | async-start | bytes 4194304 | tf_op jit(solution)/shard_map/all_to_all | solution.py:167
  83.3 4.7 %select_reduce_fusion.1 = (f32[16,512,64]{1,2,0:T(8,128)}, f32[16,512,64]{1,2,0:T(8,128)S(1)}) fusion(f32[7]{0:T(128)S(1)} %copy-done.11, s32[16,512,64]{1,2,0:T(8,128)S(1)} %get-tuple-element.38, s32[7]{0:T(128)S(1)} %and_select_fusion, s32[16,512,64]{1,2,0:T(8,128)S(1)} %get-tuple-element.37), kind=kLoop, calls=%fused_computation.1 | loop fusion | flops 20971520 | bytes 8388664 | tf_op jit(solution)/shard_map/vmap()/reduce_sum | solution.py:110
  87.9 2.7 %copy.97 = f32[16,512,64]{2,1,0:T(8,128)} copy(f32[16,512,64]{1,2,0:T(8,128)S(1)} %get-tuple-element.11) | data formatting | bytes 4194304 | tf_op jit(solution)/shard_map/vmap()/reduce_sum | solution.py:110
  90.9 17.0 %all-to-all-done = bf16[128,64,128]{2,1,0:T(8,128)(2,1)} async-done(((bf16[128,64,128]{2,1,0:T(8,128)(2,1)}), bf16[128,64,128]{2,1,0:T(8,128)(2,1)}, u32[]{:S(2)}, u32[]{:S(2)}) %all-to-all-start) | async-done | bytes 2097184 | tf_op jit(solution)/shard_map/all_to_all | solution.py:167
  108.0 2.2 convert_reduce_fusion.1
  110.2 3.6 %fusion.108 = f32[16,512,128]{1,2,0:T(8,128)S(1)} fusion(f32[16,512,64]{1,2,0:T(8,128)S(1)} %copy-done, f32[16,64,128]{2,1,0:T(8,128)S(1)} %convert_reduce_fusion.1), kind=kOutput, calls=%fused_computation.183 | convolution fusion | flops 805306368 | bytes 6815744 | tf_op jit(solution)/shard_map/vmap()/dot_general | solution.py:123
  116.1 2.5 broadcast_multiply_fusion.1
  118.6 4.1 %fusion.45 = bf16[16,64,128]{2,1,0:T(8,128)(2,1)} fusion(f32[16,512,64]{1,2,0:T(8,128)S(1)} %copy-done, f32[16,512,64]{2,1,0:T(8,128)S(1)} %get-tuple-element.30, f32[16,512,64]{2,1,0:T(8,128)S(1)} %get-tuple-element.29), kind=kOutput, calls=%fused_computation.89 | convolution fusion | flops 806486016 | bytes 6553600 | tf_op jit(solution)/shard_map/vmap()/dot_general | solution.py:117
  122.6 25.1 %all-gather.5.cloned.1.call-done = bf16[128,64,128]{2,1,0:T(8,128)(2,1)} async-done(((bf16[16,64,128]{2,1,0:T(8,128)(2,1)}), bf16[128,64,128]{2,1,0:T(8,128)(2,1)}) %all-gather.5.cloned.1.call-update) | async-done | bytes 2097168 | tf_op jit(solution)/shard_map/all_gather | solution.py:178
  147.8 4.1 %copy.99 = bf16[128,64,128]{0,1,2:T(8,128)(2,1)S(1)} copy(bf16[128,64,128]{2,1,0:T(8,128)(2,1)} %all-gather.5.cloned.1.call-done) | data formatting | bytes 4194304 | tf_op jit(solution)/shard_map/all_gather | solution.py:178
  156.6 2.9 %slice_subtract_fusion = (f32[1,1,64,64,128]{4,3,0,2,1:T(8,128)}, f32[1,1,64,64,128]{4,3,0,2,1:T(8,128)}) fusion(f32[2,2,64,64,128]{4,3,0,2,1:T(8,128)S(1)} %convolution_bitcast_fusion), kind=kLoop, calls=%fused_computation.38 | loop fusion | flops 1048576 | bytes 12582912 | tf_op jit(solution)/shard_map/sub | solution.py:96
  161.2 2.8 %sub.229 = f32[1,1,64,8192]{3,2,1,0:T(8,128)} reshape(f32[1,1,64,64,128]{4,3,0,2,1:T(8,128)} %get-tuple-element.21) | data formatting | bytes 4194304 | tf_op jit(solution)/shard_map/sub | solution.py:96
  164.0 8.8 %fusion.17 = (f32[1,1,64,8192]{3,2,1,0:T(8,128)S(1)}, f32[1,1,64,8192]{3,2,1,0:T(8,128)S(1)}) fusion(f32[1,1,64,8192]{3,2,1,0:T(8,128)} %sub.229, bf16[1,1,64,8192]{3,2,1,0:T(8,128)(2,1)S(1)} %copy-done.2, f32[1,1,64,8192]{3,2,1,0:T(8,128)S(1)} %add.275), kind=kLoop, calls=%fused_computation.34 | loop fusion | flops 3670016 | bytes 9437184 | tf_op jit(solution)/shard_map/add | solution.py:101
  173.0 6.8 %copy.103 = bf16[1,2,64,8192]{2,1,0,3:T(2,128)(2,1)} copy(bf16[1,2,64,8192]{3,2,1,0:T(8,128)(2,1)S(1)} %fusion.4) | data formatting | bytes 4194304 | tf_op jit(solution)/shard_map/convert_element_type | solution.py:179
  179.9 5.9 %reshape.702 = bf16[4,2,131072]{2,1,0:T(2,128)(2,1)} reshape(bf16[8192,1,2,64]{3,2,1,0:T(2,128)(2,1)} %bitcast.221) | data formatting | bytes 4194304
  185.8 4.7 %all-to-all-start.1 = ((bf16[4,2,131072]{2,1,0:T(2,128)(2,1)}), bf16[4,2,131072]{2,1,0:T(2,128)(2,1)S(1)}, u32[]{:S(2)}, u32[]{:S(2)}) async-start(bf16[4,2,131072]{2,1,0:T(2,128)(2,1)} %reshape.702), calls=%async_computation.1 | async-start | bytes 4194304 | tf_op jit(solution)/shard_map/all_to_all | solution.py:182
  191.2 47.9 %all-to-all-done.1 = bf16[4,2,131072]{2,1,0:T(2,128)(2,1)S(1)} async-done(((bf16[4,2,131072]{2,1,0:T(2,128)(2,1)}), bf16[4,2,131072]{2,1,0:T(2,128)(2,1)S(1)}, u32[]{:S(2)}, u32[]{:S(2)}) %all-to-all-start.1) | async-done | bytes 2097184 | tf_op jit(solution)/shard_map/all_to_all | solution.py:182
  239.1 4.0 %reshape.703 = bf16[8192,1,2,64]{3,2,1,0:T(2,128)(2,1)} reshape(bf16[4,2,131072]{2,1,0:T(2,128)(2,1)S(1)} %all-to-all-done.1) | data formatting | bytes 4194304
  243.1 7.3 %convert_reduce_fusion = f32[2,64,2048]{1,0,2:T(2,128)S(1)} fusion(bf16[2,64,4,2048]{1,0,3,2:T(2,128)(2,1)} %bitcast.222), kind=kLoop, calls=%fused_computation.2 | loop fusion | flops 1835008 | bytes 3145728 | tf_op jit(solution)/shard_map/reduce_sum | solution.py:183
  250.4 2.1 copy.105
  (64 shorter events, 22.3 us)
Async XLA Ops:
  7.2 50.8 %all-gather.3.cloned.1.call-start = ((), (), s32[]{:S(2)}) async-start(), calls=%async_computation.2 | async-start | bytes 2621440 | tf_op jit(solution)/shard_map/all_gather | solution.py:155
  12.9 47.0 %copy-start.2 = (bf16[1,1,64,8192]{3,2,1,0:T(8,128)(2,1)S(1)}, bf16[1,1,64,8192]{3,2,1,0:T(8,128)(2,1)}, u32[]{:S(2)}) copy-start(bf16[1,1,64,8192]{3,2,1,0:T(8,128)(2,1)} %param.11) | copy-start | bytes 3145732
  76.8 4.7 %copy-start.8 = (s32[1,16,512]{2,1,0:T(8,128)S(1)}, s32[1,16,512]{2,1,0:T(8,128)}, u32[]{:S(2)}) copy-start(s32[1,16,512]{2,1,0:T(8,128)} %param.17) | copy-start | bytes 98308
  76.8 4.8 %copy-start.9 = (s32[1,16,512]{2,1,0:T(8,128)S(1)}, s32[1,16,512]{2,1,0:T(8,128)}, u32[]{:S(2)}) copy-start(s32[1,16,512]{2,1,0:T(8,128)} %param.16) | copy-start | bytes 98308
  76.8 31.1 %all-to-all-start = ((bf16[128,64,128]{2,1,0:T(8,128)(2,1)}), bf16[128,64,128]{2,1,0:T(8,128)(2,1)}, u32[]{:S(2)}, u32[]{:S(2)}) async-start(bf16[128,64,128]{2,1,0:T(8,128)(2,1)} %copy.96), calls=%async_computation | async-start | bytes 4194304 | tf_op jit(solution)/shard_map/all_to_all | solution.py:167
  81.3 66.4 %all-gather.5.cloned.1.call-start = ((), (), s32[]{:S(2)}) async-start(), calls=%async_computation.3 | async-start | bytes 2359296 | tf_op jit(solution)/shard_map/all_gather | solution.py:178
  81.6 1.6 copy-start.11
  87.9 2.7 %copy-start.10 = (s32[1,16,512]{2,1,0:T(8,128)S(1)}, s32[1,16,512]{2,1,0:T(8,128)}, u32[]{:S(2)}) copy-start(s32[1,16,512]{2,1,0:T(8,128)} %param.18) | copy-start | bytes 98308
  87.9 2.7 %copy-start.12 = (f32[1,8]{1,0:T(1,128)S(1)}, f32[1,8]{1,0:T(1,128)}, u32[]{:S(2)}) copy-start(f32[1,8]{1,0:T(1,128)} %param.15) | copy-start | bytes 100
  108.0 2.2 copy-start
  113.8 0.9 copy-start.7
  113.8 2.2 copy-start.1
  114.8 3.7 %copy-start.3 = (f32[1,16,512]{2,1,0:T(8,128)}, f32[1,16,512]{2,1,0:T(8,128)S(1)}, u32[]{:S(2)}) copy-start(f32[1,16,512]{2,1,0:T(8,128)S(1)} %get-tuple-element.13) | copy-start | bytes 98308
  114.8 3.7 %copy-start.5 = (f32[1,16,512]{2,1,0:T(8,128)}, f32[1,16,512]{2,1,0:T(8,128)S(1)}, u32[]{:S(2)}) copy-start(f32[1,16,512]{2,1,0:T(8,128)S(1)} %get-tuple-element.14) | copy-start | bytes 98308
  185.8 4.7 %copy-start.4 = (f32[1,16,512]{2,1,0:T(8,128)S(1)}, f32[1,16,512]{2,1,0:T(8,128)}, u32[]{:S(2)}) copy-start(f32[1,16,512]{2,1,0:T(8,128)} %copy-done.3) | copy-start | bytes 98308
  185.8 4.7 %copy-start.6 = (f32[1,16,512]{2,1,0:T(8,128)S(1)}, f32[1,16,512]{2,1,0:T(8,128)}, u32[]{:S(2)}) copy-start(f32[1,16,512]{2,1,0:T(8,128)} %copy-done.5) | copy-start | bytes 98308
  185.8 53.3 %all-to-all-start.1 = ((bf16[4,2,131072]{2,1,0:T(2,128)(2,1)}), bf16[4,2,131072]{2,1,0:T(2,128)(2,1)S(1)}, u32[]{:S(2)}, u32[]{:S(2)}) async-start(bf16[4,2,131072]{2,1,0:T(2,128)(2,1)} %reshape.702), calls=%async_computation.1 | async-start | bytes 4194304 | tf_op jit(solution)/shard_map/all_to_all | solution.py:182
Sparse Core Ops, SparseCore 0:
  9.5 48.3 all-gather.2
  122.8 24.9 all-gather.4
where the time goes:
time: 260 us; the launch traced here: 259 us
  waiting for transfers between devices  136 us (52%)
  other arithmetic  47.9 us (18%)
  local copies, waits for them, and re-layouts  38.4 us (15%)
  between operations  15.1 us (6%)
  matrix products  12.7 us (5%)
  starting transfers between devices  9.47 us (4%)
    all_to_all x1, waiting for transfers between devices, local(): lax.all_to_all(term[None], 'layer', split_axis=3, concat_axis=0, tiled=True)  47.9 us
    all_gather x1, waiting for transfers between devices, local(): strip_data = lax.all_gather(model_strip, 'layer', axis=3, tiled=True)[0]  45 us
    all_gather x1, waiting for transfers between devices, local(): all_grids = lax.all_gather(adjoint, 'facet', axis=0, tiled=True)  25.1 us
    all_to_all x1, waiting for transfers between devices, local(): lax.all_to_all(contrib, 'facet', split_axis=0, concat_axis=0, tiled=True)  17 us
    unnamed x34, local copies, waits for them, and re-layouts  16.6 us
    unnamed x2, other arithmetic  9.45 us
    add x1, other arithmetic, backward(): image_real * cosine + image_imag * sine_part  8.78 us
    reduce_sum x1, other arithmetic, local(): gradient = jnp.sum(pieces.astype(jnp.float32), axis=0)[None]  7.26 us
  transfers between devices with their start and end apart: 4, of which 4 were waited for; matrix products, arithmetic and copies ran while one was open for 6% of the time, Pallas kernels for 0%

commit v1 on v0

--- a/solution.py
+++ b/solution.py
@@ -179,7 +179,12 @@
     term = backward(all_grids, facet_window[0], facet_shift[0], screen_angle[0, 0]).astype(
         jnp.bfloat16
     )
-    pieces = lax.all_to_all(term[None], "layer", split_axis=3, concat_axis=0, tiled=True)
+    pieces = jnp.concatenate(
+        lax.all_to_all(
+            jnp.stack(jnp.split(term[None], lax.axis_size("layer"), axis=3)), "layer", 0, 0
+        ),
+        axis=0,
+    )
     gradient = jnp.sum(pieces.astype(jnp.float32), axis=0)[None]
     return (residual_vis[None], gradient)
 

time: 260 us -> 237 us (0.912)
  local copies, waits for them, and re-layouts: 38.4 us -> 19.7 us
  other arithmetic: 47.9 us -> 43.6 us
    unnamed x34 -> x31, local copies, waits for them, and re-layouts: 16.6 us -> 4.54 us
    convert_element_type x1 -> x0, local copies, waits for them, and re-layouts: 6.85 us -> none  [local(): backward(all_grids, facet_window[0], facet_shift[0], screen_angle[0, 0])]
    reduce_sum x1, other arithmetic: 7.26 us -> 1.35 us  [local(): gradient = jnp.sum(pieces.astype(jnp.float32), axis=0)[None]]
where the time goes in v1:
time: 237 us; the launch traced here: 236 us
  waiting for transfers between devices  136 us (57%)
  other arithmetic  43.6 us (18%)
  local copies, waits for them, and re-layouts  19.7 us (8%)
  between operations  15.1 us (6%)
  matrix products  12.7 us (5%)
  starting transfers between devices  9.47 us (4%)
    all_to_all x1, waiting for transfers between devices, local(): lax.all_to_all(jnp.stack(jnp.split(term[None], lax.axis_size('layer'), ax...  47.9 us
    all_gather x1, waiting for transfers between devices, local(): strip_data = lax.all_gather(model_strip, 'layer', axis=3, tiled=True)[0]  45 us
    all_gather x1, waiting for transfers between devices, local(): all_grids = lax.all_gather(adjoint, 'facet', axis=0, tiled=True)  25.1 us
    all_to_all x1, waiting for transfers between devices, local(): lax.all_to_all(contrib, 'facet', split_axis=0, concat_axis=0, tiled=True)  17 us
    unnamed x2, other arithmetic  9.45 us
    add x1, other arithmetic, backward(): image_real * cosine + image_imag * sine_part  8.78 us
  transfers between devices with their start and end apart: 4, of which 4 were waited for; matrix products, arithmetic and copies ran while one was open for 6% of the time, Pallas kernels for 0%

profile of v1, /device:TPU:0, one launch (start us, length us, event | category | flops | bytes accessed | tf_op | source)
XLA Modules:
  0.0 236.3 jit_solution(4633682786150660480)
XLA Ops:
  8.4 1.5 reduce.4
  10.7 1.5 copy.108
  13.0 45.0 %all-gather.3.cloned.1.call-done = bf16[1,2,64,8192]{3,2,1,0:T(8,128)(2,1)} async-done(((bf16[1,2,64,2048]{3,2,1,0:T(8,128)(2,1)}), bf16[1,2,64,8192]{3,2,1,0:T(8,128)(2,1)}) %all-gather.3.cloned.1.call-update) | async-done | bytes 2097168 | tf_op jit(solution)/shard_map/all_gather | solution.py:155
  58.0 2.0 convert_element_type.139
  60.0 8.0 %fusion.51 = (bf16[8,8,64,128]{3,1,2,0:T(8,128)(2,1)S(1)}, bf16[8,8,64,128]{3,1,2,0:T(8,128)(2,1)S(1)}) fusion(f32[1,2,64,8192]{3,2,1,0:T(8,128)S(1)} %convert_element_type.139, bf16[1,1,64,8192]{3,2,1,0:T(8,128)(2,1)S(1)} %copy-done.2), kind=kLoop, calls=%fused_computation.94 | loop fusion | flops 4718592 | bytes 7340032
  73.4 3.4 %copy.82 = bf16[128,64,128]{2,1,0:T(8,128)(2,1)} copy(bf16[128,64,128]{0,1,2:T(8,128)(2,1)S(1)} %pad_maximum_fusion) | data formatting | bytes 4194304 | tf_op jit(solution)/shard_map/concatenate | solution.py:60
  76.8 4.5 %all-to-all-start = ((bf16[128,64,128]{2,1,0:T(8,128)(2,1)}), bf16[128,64,128]{2,1,0:T(8,128)(2,1)}, u32[]{:S(2)}, u32[]{:S(2)}) async-start(bf16[128,64,128]{2,1,0:T(8,128)(2,1)} %copy.82), calls=%async_computation | async-start | bytes 4194304 | tf_op jit(solution)/shard_map/all_to_all | solution.py:167
  81.6 1.6 add_select_fusion
  83.2 4.7 %select_reduce_fusion.1 = (f32[16,512,64]{1,2,0:T(8,128)}, f32[16,512,64]{1,2,0:T(8,128)S(1)}) fusion(f32[7]{0:T(128)S(1)} %copy-done.11, s32[16,512,64]{1,2,0:T(8,128)S(1)} %get-tuple-element.40, s32[7]{0:T(128)S(1)} %and_select_fusion, s32[16,512,64]{1,2,0:T(8,128)S(1)} %get-tuple-element.39), kind=kLoop, calls=%fused_computation.1 | loop fusion | flops 20971520 | bytes 8388664 | tf_op jit(solution)/shard_map/vmap()/reduce_sum | solution.py:110
  87.9 2.7 %copy.83 = f32[16,512,64]{2,1,0:T(8,128)} copy(f32[16,512,64]{1,2,0:T(8,128)S(1)} %get-tuple-element.9) | data formatting | bytes 4194304 | tf_op jit(solution)/shard_map/vmap()/reduce_sum | solution.py:110
  90.9 17.0 %all-to-all-done = bf16[128,64,128]{2,1,0:T(8,128)(2,1)} async-done(((bf16[128,64,128]{2,1,0:T(8,128)(2,1)}), bf16[128,64,128]{2,1,0:T(8,128)(2,1)}, u32[]{:S(2)}, u32[]{:S(2)}) %all-to-all-start) | async-done | bytes 2097184 | tf_op jit(solution)/shard_map/all_to_all | solution.py:167
  108.0 2.2 convert_reduce_fusion
  110.2 3.6 %fusion.108 = f32[16,512,128]{1,2,0:T(8,128)S(1)} fusion(f32[16,512,64]{1,2,0:T(8,128)S(1)} %copy-done, f32[16,64,128]{2,1,0:T(8,128)S(1)} %convert_reduce_fusion), kind=kOutput, calls=%fused_computation.188 | convolution fusion | flops 805306368 | bytes 6815744 | tf_op jit(solution)/shard_map/vmap()/dot_general | solution.py:123
  116.1 2.5 %broadcast_multiply_fusion.1 = (f32[16,512,64]{2,1,0:T(8,128)S(1)}, f32[16,512,64]{2,1,0:T(8,128)S(1)}) fusion(f32[16,512,64]{2,1,0:T(8,128)S(1)} %copy-done.1, f32[16,512]{1,0:T(8,128)S(1)} %get-tuple-element.33, f32[16,512]{1,0:T(8,128)S(1)} %get-tuple-element.34), kind=kLoop, calls=%fused_computation.79 | loop fusion | flops 1048576 | bytes 6356992 | tf_op jit(solution)/shard_map/vmap()/mul | solution.py:115
  118.6 4.1 %fusion.45 = bf16[16,64,128]{2,1,0:T(8,128)(2,1)} fusion(f32[16,512,64]{1,2,0:T(8,128)S(1)} %copy-done, f32[16,512,64]{2,1,0:T(8,128)S(1)} %get-tuple-element.28, f32[16,512,64]{2,1,0:T(8,128)S(1)} %get-tuple-element.27), kind=kOutput, calls=%fused_computation.90 | convolution fusion | flops 806486016 | bytes 6553600 | tf_op jit(solution)/shard_map/vmap()/dot_general | solution.py:117
  122.6 25.1 %all-gather.5.cloned.1.call-done = bf16[128,64,128]{2,1,0:T(8,128)(2,1)} async-done(((bf16[16,64,128]{2,1,0:T(8,128)(2,1)}), bf16[128,64,128]{2,1,0:T(8,128)(2,1)}) %all-gather.5.cloned.1.call-update) | async-done | bytes 2097168 | tf_op jit(solution)/shard_map/all_gather | solution.py:178
  147.8 4.1 %copy.85 = bf16[128,64,128]{0,1,2:T(8,128)(2,1)S(1)} copy(bf16[128,64,128]{2,1,0:T(8,128)(2,1)} %all-gather.5.cloned.1.call-done) | data formatting | bytes 4194304 | tf_op jit(solution)/shard_map/all_gather | solution.py:178
  156.6 2.9 %slice_subtract_fusion = (f32[1,1,64,64,128]{4,3,0,2,1:T(8,128)}, f32[1,1,64,64,128]{4,3,0,2,1:T(8,128)}) fusion(f32[2,2,64,64,128]{4,3,0,2,1:T(8,128)S(1)} %convolution_bitcast_fusion), kind=kLoop, calls=%fused_computation.38 | loop fusion | flops 1048576 | bytes 12582912 | tf_op jit(solution)/shard_map/sub | solution.py:96
  159.5 1.7 add.275
  161.2 2.7 %sub.229 = f32[1,1,64,8192]{3,2,1,0:T(8,128)} reshape(f32[1,1,64,64,128]{4,3,0,2,1:T(8,128)} %get-tuple-element.19) | data formatting | bytes 4194304 | tf_op jit(solution)/shard_map/sub | solution.py:96
  164.0 8.8 %fusion.17 = (f32[1,1,64,8192]{3,2,1,0:T(8,128)S(1)}, f32[1,1,64,8192]{3,2,1,0:T(8,128)S(1)}) fusion(f32[1,1,64,8192]{3,2,1,0:T(8,128)} %sub.229, bf16[1,1,64,8192]{3,2,1,0:T(8,128)(2,1)S(1)} %copy-done.2, f32[1,1,64,8192]{3,2,1,0:T(8,128)S(1)} %add.275), kind=kLoop, calls=%fused_computation.34 | loop fusion | flops 3670016 | bytes 9437184 | tf_op jit(solution)/shard_map/add | solution.py:101
  173.2 1.6 pad_maximum_fusion.1
  174.8 4.7 %all-to-all-start.1 = ((bf16[4,1,2,64,2048]{4,3,2,1,0:T(8,128)(2,1)}), bf16[4,1,2,64,2048]{4,3,2,1,0:T(8,128)(2,1)S(1)}, u32[]{:S(2)}, u32[]{:S(2)}) async-start(bf16[4,1,2,64,2048]{4,3,2,1,0:T(8,128)(2,1)} %pad_maximum_fusion.1), calls=%async_computation.1 | async-start | bytes 4194304 | tf_op jit(solution)/shard_map/all_to_all | solution.py:183
  180.2 47.9 %all-to-all-done.1 = bf16[4,1,2,64,2048]{4,3,2,1,0:T(8,128)(2,1)S(1)} async-done(((bf16[4,1,2,64,2048]{4,3,2,1,0:T(8,128)(2,1)}), bf16[4,1,2,64,2048]{4,3,2,1,0:T(8,128)(2,1)S(1)}, u32[]{:S(2)}, u32[]{:S(2)}) %all-to-all-start.1) | async-done | bytes 2097184 | tf_op jit(solution)/shard_map/all_to_all | solution.py:183
  (62 shorter events, 17.4 us)
Async XLA Ops:
  7.2 50.8 %all-gather.3.cloned.1.call-start = ((), (), s32[]{:S(2)}) async-start(), calls=%async_computation.2 | async-start | bytes 2621440 | tf_op jit(solution)/shard_map/all_gather | solution.py:155
  12.9 47.0 %copy-start.2 = (bf16[1,1,64,8192]{3,2,1,0:T(8,128)(2,1)S(1)}, bf16[1,1,64,8192]{3,2,1,0:T(8,128)(2,1)}, u32[]{:S(2)}) copy-start(bf16[1,1,64,8192]{3,2,1,0:T(8,128)(2,1)} %param.11) | copy-start | bytes 3145732
  76.8 4.7 %copy-start.8 = (s32[1,16,512]{2,1,0:T(8,128)S(1)}, s32[1,16,512]{2,1,0:T(8,128)}, u32[]{:S(2)}) copy-start(s32[1,16,512]{2,1,0:T(8,128)} %param.17) | copy-start | bytes 98308
  76.8 4.8 %copy-start.9 = (s32[1,16,512]{2,1,0:T(8,128)S(1)}, s32[1,16,512]{2,1,0:T(8,128)}, u32[]{:S(2)}) copy-start(s32[1,16,512]{2,1,0:T(8,128)} %param.16) | copy-start | bytes 98308
  76.8 31.1 %all-to-all-start = ((bf16[128,64,128]{2,1,0:T(8,128)(2,1)}), bf16[128,64,128]{2,1,0:T(8,128)(2,1)}, u32[]{:S(2)}, u32[]{:S(2)}) async-start(bf16[128,64,128]{2,1,0:T(8,128)(2,1)} %copy.82), calls=%async_computation | async-start | bytes 4194304 | tf_op jit(solution)/shard_map/all_to_all | solution.py:167
  81.3 66.4 %all-gather.5.cloned.1.call-start = ((), (), s32[]{:S(2)}) async-start(), calls=%async_computation.3 | async-start | bytes 2359296 | tf_op jit(solution)/shard_map/all_gather | solution.py:178
  81.6 1.6 copy-start.11
  87.9 2.7 %copy-start.10 = (s32[1,16,512]{2,1,0:T(8,128)S(1)}, s32[1,16,512]{2,1,0:T(8,128)}, u32[]{:S(2)}) copy-start(s32[1,16,512]{2,1,0:T(8,128)} %param.18) | copy-start | bytes 98308
  87.9 2.7 %copy-start.12 = (f32[1,8]{1,0:T(1,128)S(1)}, f32[1,8]{1,0:T(1,128)}, u32[]{:S(2)}) copy-start(f32[1,8]{1,0:T(1,128)} %param.15) | copy-start | bytes 100
  108.0 2.2 copy-start
  113.8 0.9 copy-start.7
  113.8 2.2 copy-start.1
  114.8 3.7 %copy-start.3 = (f32[1,16,512]{2,1,0:T(8,128)}, f32[1,16,512]{2,1,0:T(8,128)S(1)}, u32[]{:S(2)}) copy-start(f32[1,16,512]{2,1,0:T(8,128)S(1)} %get-tuple-element.11) | copy-start | bytes 98308
  114.8 3.7 %copy-start.5 = (f32[1,16,512]{2,1,0:T(8,128)}, f32[1,16,512]{2,1,0:T(8,128)S(1)}, u32[]{:S(2)}) copy-start(f32[1,16,512]{2,1,0:T(8,128)S(1)} %get-tuple-element.12) | copy-start | bytes 98308
  174.8 4.7 %copy-start.4 = (f32[1,16,512]{2,1,0:T(8,128)S(1)}, f32[1,16,512]{2,1,0:T(8,128)}, u32[]{:S(2)}) copy-start(f32[1,16,512]{2,1,0:T(8,128)} %copy-done.3) | copy-start | bytes 98308
  174.8 4.7 %copy-start.6 = (f32[1,16,512]{2,1,0:T(8,128)S(1)}, f32[1,16,512]{2,1,0:T(8,128)}, u32[]{:S(2)}) copy-start(f32[1,16,512]{2,1,0:T(8,128)} %copy-done.5) | copy-start | bytes 98308
  174.8 53.3 %all-to-all-start.1 = ((bf16[4,1,2,64,2048]{4,3,2,1,0:T(8,128)(2,1)}), bf16[4,1,2,64,2048]{4,3,2,1,0:T(8,128)(2,1)S(1)}, u32[]{:S(2)}, u32[]{:S(2)}) async-start(bf16[4,1,2,64,2048]{4,3,2,1,0:T(8,128)(2,1)} %pad_maximum_fusion.1), calls=%async_computation.1 | async-start | bytes 4194304 | tf_op jit(solution)/shard_map/all_to_all | solution.py:183
Sparse Core Ops, SparseCore 0:
  9.5 48.3 all-gather.2
  122.8 24.9 all-gather.4
